TPU v7x, 32 devices: a whole 2x2x4 slice. The times are simulated.
32 devices in a mesh: rep: 4 (over y, core), shard: 8 (over z, x).
Axes of the slice: x: 2, y: 2, z: 4, core: 2. Of those that a mesh axis runs over, the one named last changes fastest.
Arguments:
- hidden: bfloat16 [14336, 3584], P(('rep', 'shard')), may hold values from -144 to 144
- cotangent: bfloat16 [14336, 1024], P(('rep', 'shard')), may hold values from -6 to 6
- seq_ids: int32 [32, 448], P(('rep', 'shard')), may hold values from 0 to 3, as said below
- response_mask: int32 [32, 448], P(('rep', 'shard')), may hold values from 0 to 1, as said below
- group_ids: int32 [32, 4], P(('rep', 'shard')), may hold values from 0 to 15
- rewards: float32 [32, 4], P(('rep', 'shard')), may hold values from -6 to 6
- new_logp: float32 [32, 448], P(('rep', 'shard')), may hold values from -1.5 to -0.1
- old_logp: float32 [32, 448], P(('rep', 'shard')), may hold values from -1.5 to -0.1
- ref_logp: float32 [32, 448], P(('rep', 'shard')), may hold values from -1.5 to -0.1
- master: float32 [3, 3584, 1024], P(None, 'shard'), may hold values from -6 to 6
Outputs:
- new_master: float32 [3584, 1024], P('shard')
- rollout: bfloat16 [3, 3584, 2048], P(None, None, 'shard')
Inputs may be any that keep to these rules, and one draw needn't show every extreme that they name: `seq_ids`: each row numbers its device's 4 sequences in token order, never falling, each with one token or more. `response_mask`: within a sequence, prompt tokens come before response tokens; a sequence may have no response tokens.
All inputs are finite; a program needn't handle non-finite values.
Results may differ from a plain program's by a relative error of at most 0.0095.
Values may be sent and summed in bfloat16 or wider, within the bound.
A program may use at most 128 MiB of HBM per device.

v0:
```python
import jax
import jax.numpy as jnp
from jax import lax
from jax.sharding import PartitionSpec as P

HEAD = 128
KV_HEADS = 4
TP = 8
SEQ_DEV = 4


def token_coef(seq_row, mask_row, adv_row, new_row, old_row, ref_row):
    onehot = (seq_row[:, None] == jnp.arange(SEQ_DEV, dtype=jnp.int32)[None, :]).astype(jnp.float32)
    maskf = mask_row.astype(jnp.float32)
    lengths = jnp.maximum(jnp.dot(maskf, onehot, precision=lax.Precision.HIGHEST), 1.0)
    tok_len = jnp.dot(onehot, lengths, precision=lax.Precision.HIGHEST)
    tok_adv = jnp.dot(onehot, adv_row, precision=lax.Precision.HIGHEST)
    surrogate = -tok_adv * jnp.exp(new_row - old_row) + 0.2 * (1.0 - jnp.exp(ref_row - new_row))
    return maskf / tok_len * surrogate


def group_advantage(group_flat, reward_flat, stats):
    groups = stats.shape[1]
    onehot = (group_flat[:, None] == jnp.arange(groups, dtype=jnp.int32)[None, :]).astype(
        jnp.float32
    )
    count = jnp.maximum(stats[0], 1.0)
    mean = stats[1] / count
    spread = jnp.sqrt(jnp.maximum(stats[2] / count - mean * mean, 0.0))
    tok_mean = jnp.dot(onehot, mean, precision=lax.Precision.HIGHEST)
    tok_std = jnp.dot(onehot, jnp.maximum(spread, 0.5), precision=lax.Precision.HIGHEST)
    return (reward_flat - tok_mean) / tok_std


def group_sums(group_flat, reward_flat, groups):
    onehot = (group_flat[:, None] == jnp.arange(groups, dtype=jnp.int32)[None, :]).astype(
        jnp.float32
    )
    values = jnp.stack([jnp.ones_like(reward_flat), reward_flat, reward_flat * reward_flat], axis=0)
    return jnp.dot(values, onehot, precision=lax.Precision.HIGHEST)


def rounded(term):
    return lax.optimization_barrier(term.astype(jnp.bfloat16)).astype(jnp.float32)


def rollout_blocks(weights):
    layer_count = weights.shape[0]
    row_count = weights.shape[1]
    paired = weights.reshape(layer_count, row_count, 2, KV_HEADS, HEAD).transpose(0, 1, 3, 2, 4)
    paired = paired.reshape(layer_count, row_count, KV_HEADS, 2 * HEAD)
    by_rank = jnp.repeat(paired, TP // KV_HEADS, axis=2)
    copies = jnp.tile(by_rank, (1, 1, lax.axis_size("shard") // TP, 1))
    return copies.reshape(layer_count, row_count, lax.axis_size("shard") * 2 * HEAD)


def per_device(
    hidden,
    cotangent,
    seq_ids,
    response_mask,
    group_ids,
    rewards,
    new_logp,
    old_logp,
    ref_logp,
    master,
):
    n_rep = lax.axis_size("rep")
    n_shard = lax.axis_size("shard")
    groups = n_rep * n_shard * SEQ_DEV // 8
    rest_cols = lax.all_to_all(
        rollout_blocks(master[1:].astype(jnp.bfloat16)),
        "shard",
        split_axis=2,
        concat_axis=1,
        tiled=True,
    )
    local_sums = group_sums(group_ids[0], rewards[0], groups)
    stats = lax.psum(local_sums, ("rep", "shard"))
    advantage = group_advantage(group_ids[0], rewards[0], stats)
    coef = token_coef(
        seq_ids[0], response_mask[0], advantage, new_logp[0], old_logp[0], ref_logp[0]
    )
    delta = (coef[:, None] * cotangent.astype(jnp.float32)).astype(jnp.bfloat16)
    feature_count = hidden.shape[1]
    partial_value = lax.psum_scatter(
        rounded(
            lax.dot_general(
                hidden, delta, (((0,), (0,)), ((), ())), preferred_element_type=jnp.float32
            )
        ).astype(jnp.bfloat16),
        "shard",
        scatter_dimension=0,
        tiled=True,
    )
    grad = lax.psum(partial_value, "rep").astype(jnp.float32)
    squares = lax.psum(jnp.sum(grad * grad), "shard")
    rms = jnp.sqrt(squares / (feature_count * grad.shape[1]) + 1e-06)
    new_master = master[0] - 0.5 * grad / rms
    first_cols = lax.all_to_all(
        rollout_blocks(new_master[None].astype(jnp.bfloat16)),
        "shard",
        split_axis=2,
        concat_axis=1,
        tiled=True,
    )
    rollout = jnp.concatenate([first_cols, rest_cols], axis=0)
    return (new_master, rollout)


def solution(mesh):
    in_specs = (
        P(("rep", "shard"), None),
        P(("rep", "shard"), None),
        P(("rep", "shard"), None),
        P(("rep", "shard"), None),
        P(("rep", "shard"), None),
        P(("rep", "shard"), None),
        P(("rep", "shard"), None),
        P(("rep", "shard"), None),
        P(("rep", "shard"), None),
        P(None, "shard", None),
    )
    out_specs = (P("shard", None), P(None, None, "shard"))
    return jax.shard_map(
        per_device, mesh=mesh, in_specs=in_specs, out_specs=out_specs, check_vma=False
    )
```

profile of v0, /device:TPU:0, one launch (start us, length us, event | category | flops | bytes accessed | tf_op | source)
XLA Modules:
  0.0 468.4 jit_solution(8274017862780211825)
XLA Ops:
  7.2 0.0 copy-start
  7.2 0.0 reduce-scatter.4.cloned.1.call-start
  7.2 0.8 mul.39
  8.1 1.0 fusion.15
  9.0 41.9 %psum.21 = f32[3,16]{1,0:T(4,128)S(1)} all-reduce(f32[3,16]{1,0:T(4,128)S(1)} %fusion.15), channel_id=1, replica_groups=mesh['rep'=4,'shard'=8] {'rep','shard'}, use_global_device_ids=true, to_apply=%region_0.0 | all-reduce | flops 48 | bytes 384 | tf_op jit(solution)/shard_map/psum | solution.py:80
  51.0 0.8 convolution_bitcast_fusion
  51.8 0.9 fusion.8
  52.7 0.7 convert_element_type.31
  53.4 0.9 fusion.5
  54.3 1.0 fusion.10
  55.3 1.0 fusion.11
  56.3 0.8 subtract_exponential_fusion
  57.1 0.0 copy-done
  57.1 7.5 %fusion = bf16[3584,1024]{0,1:T(8,128)(2,1)} fusion(bf16[448,3584]{1,0:T(8,128)(2,1)S(1)} %copy-done, bf16[448,1024]{1,0:T(8,128)(2,1)} %param.11, f32[448]{0:T(512)S(1)} %add_multiply_fusion), kind=kOutput, calls=%fused_computation.1 | convolution fusion | flops 3293380608 | bytes 11470592 | tf_op jit(solution)/shard_map/dot_general | solution.py:89
  64.6 10.4 %copy.47 = bf16[3584,1024]{1,0:T(8,128)(2,1)} copy(bf16[3584,1024]{0,1:T(8,128)(2,1)} %fusion) | data formatting | bytes 14680064
  75.0 0.0 reduce-scatter.4.cloned.1.call-update
  75.0 2.3 slice.36
  77.4 2.3 reshape.41
  79.6 5.7 %copy.49 = bf16[2,448,2,4,128]{1,0,4,2,3:T(2,128)(2,1)S(1)} copy(bf16[2,448,2,4,128]{4,3,2,1,0:T(4,128)(2,1)} %reshape.41) | data formatting | bytes 3670016 | tf_op jit(solution)/shard_map/transpose | solution.py:50
  85.3 4.2 broadcast_in_dim.15
  89.5 5.3 %all-to-all-start.1 = ((bf16[2,448,2048]{1,0,2:T(2,128)(2,1)}), bf16[2,448,2048]{1,0,2:T(2,128)(2,1)}, u32[]{:S(2)}, u32[]{:S(2)}) async-start(bf16[2,448,2048]{1,0,2:T(2,128)(2,1)} %bitcast.83), calls=%async_computation.1 | async-start | bytes 8388608 | tf_op jit(solution)/shard_map/all_to_all | solution.py:72
  94.8 0.0 all-reduce.2.cloned.1.call-start
  94.9 188.3 %reduce-scatter.4.cloned.1.call-done = bf16[448,1024]{1,0:T(8,128)(2,1)} async-done(((bf16[3584,1024]{1,0:T(8,128)(2,1)}), bf16[448,1024]{1,0:T(8,128)(2,1)}) %reduce-scatter.4.cloned.1.call-update) | async-done | bytes 917520
  283.2 2.2 copy.48
  285.4 0.0 all-reduce.2.cloned.1.call-update
  285.4 0.0 slice-start
  285.4 36.1 %all-reduce.2.cloned.1.call-done = bf16[448,1024]{0,1:T(8,128)(2,1)} async-done(((bf16[448,1024]{0,1:T(8,128)(2,1)}), bf16[448,1024]{0,1:T(8,128)(2,1)}) %all-reduce.2.cloned.1.call-update) | async-done | bytes 917520 | tf_op jit(solution)/shard_map/psum | solution.py:97
  321.5 2.4 fusion.3
  323.9 0.0 slice-done
  323.9 0.0 copy-start.3
  323.9 1.9 copy.51
  325.7 22.1 %psum.23 = f32[]{:T(128)} all-reduce(f32[]{:T(128)} %fusion.3), channel_id=1, replica_groups=mesh['rep'=4,'shard'=8] {'shard'}, use_global_device_ids=true, to_apply=%region_4.0 | all-reduce | flops 1 | bytes 8 | tf_op jit(solution)/shard_map/psum | solution.py:98
  348.6 0.0 copy-done.3
  348.6 3.0 fusion.36
  351.6 3.6 copy.33
  355.2 2.7 reshape.40
  357.9 0.7 copy.34
  358.6 2.5 broadcast_in_dim.6
  361.1 5.3 %broadcast_in_dim.14 = bf16[1,448,2048]{2,1,0:T(8,128)(2,1)} reshape(bf16[448,4,2,256]{3,2,1,0:T(2,128)(2,1)} %broadcast_in_dim.6) | data formatting | bytes 3670016 | tf_op jit(solution)/shard_map/broadcast_in_dim | solution.py:52
  366.4 10.7 %copy.35 = bf16[1,448,2048]{1,0,2:T(2,128)(2,1)} copy(bf16[1,448,2048]{2,1,0:T(8,128)(2,1)} %broadcast_in_dim.14) | data formatting | bytes 3670016 | tf_op jit(solution)/shard_map/broadcast_in_dim | solution.py:52
  377.1 0.5 broadcast.50
  377.6 15.4 %reduce = bf16[2048,448]{1,0:T(8,128)(2,1)} reduce(bf16[2048,1,448]{2,1,0:T(2,128)(2,1)} %bitcast.84, bf16[]{:T(256)} %broadcast.50), dimensions={1}, to_apply=%bitcast.77.reduce_sub_computation | reduce | bytes 3670018
  393.1 6.8 %reshape.57 = bf16[8,2,57344]{2,1,0:T(2,128)(2,1)} reshape(bf16[2048,448]{1,0:T(8,128)(2,1)} %reduce) | data formatting | bytes 3670016
  399.8 0.0 all-to-all-done.1
  399.8 4.3 all-to-all-start
  404.2 11.1 %copy.46 = bf16[2,448,8,256]{3,1,2,0:T(8,128)(2,1)} copy(bf16[2,448,8,256]{1,0,3,2:T(2,128)(2,1)} %bitcast.27) | data formatting | bytes 7340032 | tf_op jit(solution)/shard_map/all_to_all | solution.py:72
  415.3 1.7 copy.42
  417.0 25.9 %all-to-all-done = bf16[8,2,57344]{2,1,0:T(2,128)(2,1)} async-done(((bf16[8,2,57344]{2,1,0:T(2,128)(2,1)}), bf16[8,2,57344]{2,1,0:T(2,128)(2,1)}, u32[]{:S(2)}, u32[]{:S(2)}) %all-to-all-start) | async-done | bytes 1835040 | tf_op jit(solution)/shard_map/all_to_all | solution.py:101
  442.9 7.2 %reshape.58 = bf16[2048,1,448]{2,1,0:T(2,128)(2,1)} reshape(bf16[8,2,57344]{2,1,0:T(2,128)(2,1)} %all-to-all-done) | data formatting | bytes 3670016
  450.1 2.8 copy.50
  452.9 3.0 copy.43
  455.8 0.0 copy-start.2
  455.8 2.0 copy.37
  457.9 0.6 copy-done.2
  458.4 0.0 copy-start.1
  458.4 2.9 pad_maximum_fusion
  461.3 0.2 copy-done.1
  (3 shorter events, 0.0 us)
Async XLA Ops:
  7.2 49.9 %copy-start = (bf16[448,3584]{1,0:T(8,128)(2,1)S(1)}, bf16[448,3584]{1,0:T(8,128)(2,1)}, u32[]{:S(2)}) copy-start(bf16[448,3584]{1,0:T(8,128)(2,1)} %param.10) | copy-start | bytes 9633796
  7.2 276.0 %reduce-scatter.4.cloned.1.call-start = ((), (), s32[]{:S(2)}) async-start(), calls=%async_computation.4 | async-start | bytes 8257536
  89.5 310.4 %all-to-all-start.1 = ((bf16[2,448,2048]{1,0,2:T(2,128)(2,1)}), bf16[2,448,2048]{1,0,2:T(2,128)(2,1)}, u32[]{:S(2)}, u32[]{:S(2)}) async-start(bf16[2,448,2048]{1,0,2:T(2,128)(2,1)} %bitcast.83), calls=%async_computation.1 | async-start | bytes 8388608 | tf_op jit(solution)/shard_map/all_to_all | solution.py:72
  94.8 226.7 %all-reduce.2.cloned.1.call-start = ((), (), s32[]{:S(2)}) async-start(), calls=%async_computation.3 | async-start | bytes 2097152 | tf_op jit(solution)/shard_map/psum | solution.py:97
  285.4 38.5 %slice-start = ((f32[3,448,1024]{2,1,0:T(8,128)}), f32[1,448,1024]{2,1,0:T(8,128)S(1)}, s32[]{:S(2)}) async-start(f32[3,448,1024]{2,1,0:T(8,128)} %param.19), calls=%async_computation.5 | async-start | bytes 3670016 | tf_op jit(solution)/shard_map/slice | solution.py:100
  323.9 24.7 %copy-start.3 = (bf16[448,1024]{0,1:T(8,128)(2,1)S(1)}, bf16[448,1024]{0,1:T(8,128)(2,1)}, u32[]{:S(2)}) copy-start(bf16[448,1024]{0,1:T(8,128)(2,1)} %all-reduce.2.cloned.1.call-done) | copy-start | bytes 2752516
  399.8 43.1 %all-to-all-start = ((bf16[8,2,57344]{2,1,0:T(2,128)(2,1)}), bf16[8,2,57344]{2,1,0:T(2,128)(2,1)}, u32[]{:S(2)}, u32[]{:S(2)}) async-start(bf16[8,2,57344]{2,1,0:T(2,128)(2,1)} %reshape.57), calls=%async_computation | async-start | bytes 3670016 | tf_op jit(solution)/shard_map/all_to_all | solution.py:101
  455.8 2.6 copy-start.2
  458.4 3.1 copy-start.1
Sparse Core Ops, SparseCore 0:
  75.2 207.9 reduce-scatter.3
  286.1 35.3 all-reduce.1
where the time goes:
time: 470 us; the launch traced here: 468 us
  waiting for transfers between devices  250 us (53%)
  local copies, waits for them, and re-layouts  90.3 us (19%)
  blocking collectives  64.1 us (14%)
  other arithmetic  26 us (6%)
  between operations  14.8 us (3%)
  matrix products  13.1 us (3%)
  starting transfers between devices  9.74 us (2%)
    unnamed x3, waiting for transfers between devices  188 us
    psum x1, blocking collectives, per_device(): stats = lax.psum(local_sums, ('rep', 'shard'))  41.9 us
    psum x1, waiting for transfers between devices, per_device(): grad = lax.psum(partial_value, 'rep').astype(jnp.float32)  36.1 us
    unnamed x16, local copies, waits for them, and re-layouts  34.2 us
    all_to_all x1, waiting for transfers between devices, per_device(): lax.all_to_all(rollout_blocks(new_master[None].astype(jnp.bfloat16)), 'sh...  25.9 us
    broadcast_in_dim x4, local copies, waits for them, and re-layouts, rollout_blocks(): by_rank = jnp.repeat(paired, TP // KV_HEADS, axis=2)  22.7 us
    psum x1, blocking collectives, per_device(): squares = lax.psum(jnp.sum(grad * grad), 'shard')  22.1 us
    unnamed x1, other arithmetic  15.4 us
  transfers between devices with their start and end apart: 4, of which 3 were waited for; matrix products, arithmetic and copies ran while one was open for 18% of the time, Pallas kernels for 0%

commit v1 on v0

--- a/solution.py
+++ b/solution.py
@@ -77,7 +77,7 @@
         tiled=True,
     )
     local_sums = group_sums(group_ids[0], rewards[0], groups)
-    stats = lax.psum(local_sums, ("rep", "shard"))
+    stats = lax.psum(lax.psum(local_sums, "shard"), "rep")
     advantage = group_advantage(group_ids[0], rewards[0], stats)
     coef = token_coef(
         seq_ids[0], response_mask[0], advantage, new_logp[0], old_logp[0], ref_logp[0]

time: 470 us -> 450 us (0.957)
  blocking collectives: 64.1 us -> 50.9 us
  waiting for transfers between devices: 250 us -> 244 us
    psum x1 -> x2, blocking collectives: 41.9 us -> 28.8 us  [per_device(): stats = lax.psum(lax.psum(local_sums, 'shard'), 'rep')]
    unnamed x3, waiting for transfers between devices: 188 us -> 182 us
  transfers between devices with their start and end apart: 4 -> 4, of which waited for: 3 -> 3; matrix products, arithmetic and copies ran while one was open for 18% -> 19% of each run, Pallas kernels for 0% -> 0%
where the time goes in v1:
time: 450 us; the launch traced here: 448 us
  waiting for transfers between devices  244 us (54%)
  local copies, waits for them, and re-layouts  90.2 us (20%)
  blocking collectives  50.9 us (11%)
  other arithmetic  26.1 us (6%)
  between operations  14.8 us (3%)
  matrix products  13.2 us (3%)
  starting transfers between devices  8.95 us (2%)
    unnamed x3, waiting for transfers between devices  182 us
    psum x1, waiting for transfers between devices, per_device(): grad = lax.psum(partial_value, 'rep').astype(jnp.float32)  36.1 us
    unnamed x16, local copies, waits for them, and re-layouts  34.2 us
    psum x2, blocking collectives, per_device(): stats = lax.psum(lax.psum(local_sums, 'shard'), 'rep')  28.8 us
    all_to_all x1, waiting for transfers between devices, per_device(): lax.all_to_all(rollout_blocks(new_master[None].astype(jnp.bfloat16)), 'sh...  25.9 us
    broadcast_in_dim x4, local copies, waits for them, and re-layouts, rollout_blocks(): by_rank = jnp.repeat(paired, TP // KV_HEADS, axis=2)  22.6 us
    psum x1, blocking collectives, per_device(): squares = lax.psum(jnp.sum(grad * grad), 'shard')  22.1 us
    unnamed x1, other arithmetic  15.4 us
  transfers between devices with their start and end apart: 4, of which 3 were waited for; matrix products, arithmetic and copies ran while one was open for 19% of the time, Pallas kernels for 0%

profile of v1, /device:TPU:0, one launch (start us, length us, event | category | flops | bytes accessed | tf_op | source)
XLA Modules:
  0.0 447.9 jit_solution(14015395834165962103)
XLA Ops:
  7.2 0.0 copy-start
  7.2 0.0 reduce-scatter.4.cloned.1.call-start
  7.2 0.8 mul.39
  8.1 1.0 fusion.15
  9.0 23.1 %psum.28 = f32[3,16]{1,0:T(4,128)S(1)} all-reduce(f32[3,16]{1,0:T(4,128)S(1)} %fusion.15), channel_id=1, replica_groups=mesh['rep'=4,'shard'=8] {'shard'}, use_global_device_ids=true, to_apply=%region_0.0 | all-reduce | flops 48 | bytes 384 | tf_op jit(solution)/shard_map/psum | solution.py:80
  32.1 5.6 %psum.29 = f32[3,16]{1,0:T(4,128)S(1)} all-reduce(f32[3,16]{1,0:T(4,128)S(1)} %psum.28), channel_id=1, replica_groups=mesh['rep'=4,'shard'=8] {'rep'}, use_global_device_ids=true, to_apply=%region_1.0 | all-reduce | flops 48 | bytes 384 | tf_op jit(solution)/shard_map/psum | solution.py:80
  37.8 0.8 convolution_bitcast_fusion
  38.6 0.9 fusion.8
  39.5 0.7 convert_element_type.31
  40.2 0.9 fusion.5
  41.1 1.0 fusion.10
  42.1 1.0 fusion.11
  43.1 0.8 subtract_exponential_fusion
  43.9 0.0 copy-done
  43.9 7.5 %fusion = bf16[3584,1024]{0,1:T(8,128)(2,1)} fusion(bf16[448,3584]{1,0:T(8,128)(2,1)S(1)} %copy-done, bf16[448,1024]{1,0:T(8,128)(2,1)} %param.11, f32[448]{0:T(512)S(1)} %add_multiply_fusion), kind=kOutput, calls=%fused_computation.1 | convolution fusion | flops 3293380608 | bytes 11470592 | tf_op jit(solution)/shard_map/dot_general | solution.py:89
  51.5 10.4 %copy.47 = bf16[3584,1024]{1,0:T(8,128)(2,1)} copy(bf16[3584,1024]{0,1:T(8,128)(2,1)} %fusion) | data formatting | bytes 14680064
  61.9 0.0 reduce-scatter.4.cloned.1.call-update
  61.9 2.3 slice.36
  64.2 2.3 reshape.41
  66.5 5.7 %copy.49 = bf16[2,448,2,4,128]{1,0,4,2,3:T(2,128)(2,1)S(1)} copy(bf16[2,448,2,4,128]{4,3,2,1,0:T(4,128)(2,1)} %reshape.41) | data formatting | bytes 3670016 | tf_op jit(solution)/shard_map/transpose | solution.py:50
  72.2 4.2 broadcast_in_dim.15
  76.4 4.5 %all-to-all-start.1 = ((bf16[2,448,2048]{1,0,2:T(2,128)(2,1)}), bf16[2,448,2048]{1,0,2:T(2,128)(2,1)}, u32[]{:S(2)}, u32[]{:S(2)}) async-start(bf16[2,448,2048]{1,0,2:T(2,128)(2,1)} %bitcast.83), calls=%async_computation.1 | async-start | bytes 8388608 | tf_op jit(solution)/shard_map/all_to_all | solution.py:72
  80.9 0.0 all-reduce.2.cloned.1.call-start
  81.0 181.8 %reduce-scatter.4.cloned.1.call-done = bf16[448,1024]{1,0:T(8,128)(2,1)} async-done(((bf16[3584,1024]{1,0:T(8,128)(2,1)}), bf16[448,1024]{1,0:T(8,128)(2,1)}) %reduce-scatter.4.cloned.1.call-update) | async-done | bytes 917520
  262.8 2.2 copy.48
  265.0 0.0 all-reduce.2.cloned.1.call-update
  265.0 0.0 slice-start
  265.0 36.1 %all-reduce.2.cloned.1.call-done = bf16[448,1024]{0,1:T(8,128)(2,1)} async-done(((bf16[448,1024]{0,1:T(8,128)(2,1)}), bf16[448,1024]{0,1:T(8,128)(2,1)}) %all-reduce.2.cloned.1.call-update) | async-done | bytes 917520 | tf_op jit(solution)/shard_map/psum | solution.py:97
  301.1 2.4 fusion.3
  303.5 0.0 slice-done
  303.5 0.0 copy-start.3
  303.5 1.9 copy.51
  305.3 22.1 %psum.31 = f32[]{:T(128)} all-reduce(f32[]{:T(128)} %fusion.3), channel_id=1, replica_groups=mesh['rep'=4,'shard'=8] {'shard'}, use_global_device_ids=true, to_apply=%region_5.0 | all-reduce | flops 1 | bytes 8 | tf_op jit(solution)/shard_map/psum | solution.py:98
  328.2 0.0 copy-done.3
  328.2 3.0 fusion.36
  331.2 3.6 copy.33
  334.8 2.7 reshape.40
  337.5 0.7 copy.34
  338.2 2.5 broadcast_in_dim.6
  340.7 5.3 %broadcast_in_dim.14 = bf16[1,448,2048]{2,1,0:T(8,128)(2,1)} reshape(bf16[448,4,2,256]{3,2,1,0:T(2,128)(2,1)} %broadcast_in_dim.6) | data formatting | bytes 3670016 | tf_op jit(solution)/shard_map/broadcast_in_dim | solution.py:52
  346.0 10.7 %copy.35 = bf16[1,448,2048]{1,0,2:T(2,128)(2,1)} copy(bf16[1,448,2048]{2,1,0:T(8,128)(2,1)} %broadcast_in_dim.14) | data formatting | bytes 3670016 | tf_op jit(solution)/shard_map/broadcast_in_dim | solution.py:52
  356.7 0.5 broadcast.50
  357.2 15.4 %reduce = bf16[2048,448]{1,0:T(8,128)(2,1)} reduce(bf16[2048,1,448]{2,1,0:T(2,128)(2,1)} %bitcast.84, bf16[]{:T(256)} %broadcast.50), dimensions={1}, to_apply=%bitcast.77.reduce_sub_computation | reduce | bytes 3670018
  372.6 6.8 %reshape.57 = bf16[8,2,57344]{2,1,0:T(2,128)(2,1)} reshape(bf16[2048,448]{1,0:T(8,128)(2,1)} %reduce) | data formatting | bytes 3670016
  379.4 0.0 all-to-all-done.1
  379.4 4.3 all-to-all-start
  383.7 11.1 %copy.46 = bf16[2,448,8,256]{3,1,2,0:T(8,128)(2,1)} copy(bf16[2,448,8,256]{1,0,3,2:T(2,128)(2,1)} %bitcast.27) | data formatting | bytes 7340032 | tf_op jit(solution)/shard_map/all_to_all | solution.py:72
  394.8 1.7 copy.42
  396.6 25.9 %all-to-all-done = bf16[8,2,57344]{2,1,0:T(2,128)(2,1)} async-done(((bf16[8,2,57344]{2,1,0:T(2,128)(2,1)}), bf16[8,2,57344]{2,1,0:T(2,128)(2,1)}, u32[]{:S(2)}, u32[]{:S(2)}) %all-to-all-start) | async-done | bytes 1835040 | tf_op jit(solution)/shard_map/all_to_all | solution.py:101
  422.5 7.2 %reshape.58 = bf16[2048,1,448]{2,1,0:T(2,128)(2,1)} reshape(bf16[8,2,57344]{2,1,0:T(2,128)(2,1)} %all-to-all-done) | data formatting | bytes 3670016
  429.6 2.8 copy.50
  432.4 3.0 copy.43
  435.4 0.0 copy-start.2
  435.4 2.0 copy.37
  437.4 0.6 copy-done.2
  438.0 0.0 copy-start.1
  438.0 2.9 pad_maximum_fusion
  440.9 0.2 copy-done.1
  (3 shorter events, 0.0 us)
Async XLA Ops:
  7.2 36.8 %copy-start = (bf16[448,3584]{1,0:T(8,128)(2,1)S(1)}, bf16[448,3584]{1,0:T(8,128)(2,1)}, u32[]{:S(2)}) copy-start(bf16[448,3584]{1,0:T(8,128)(2,1)} %param.10) | copy-start | bytes 9633796
  7.2 255.6 %reduce-scatter.4.cloned.1.call-start = ((), (), s32[]{:S(2)}) async-start(), calls=%async_computation.4 | async-start | bytes 8257536
  76.4 303.0 %all-to-all-start.1 = ((bf16[2,448,2048]{1,0,2:T(2,128)(2,1)}), bf16[2,448,2048]{1,0,2:T(2,128)(2,1)}, u32[]{:S(2)}, u32[]{:S(2)}) async-start(bf16[2,448,2048]{1,0,2:T(2,128)(2,1)} %bitcast.83), calls=%async_computation.1 | async-start | bytes 8388608 | tf_op jit(solution)/shard_map/all_to_all | solution.py:72
  80.9 220.2 %all-reduce.2.cloned.1.call-start = ((), (), s32[]{:S(2)}) async-start(), calls=%async_computation.3 | async-start | bytes 2097152 | tf_op jit(solution)/shard_map/psum | solution.py:97
  265.0 38.4 %slice-start = ((f32[3,448,1024]{2,1,0:T(8,128)}), f32[1,448,1024]{2,1,0:T(8,128)S(1)}, s32[]{:S(2)}) async-start(f32[3,448,1024]{2,1,0:T(8,128)} %param.19), calls=%async_computation.5 | async-start | bytes 3670016 | tf_op jit(solution)/shard_map/slice | solution.py:100
  303.5 24.7 %copy-start.3 = (bf16[448,1024]{0,1:T(8,128)(2,1)S(1)}, bf16[448,1024]{0,1:T(8,128)(2,1)}, u32[]{:S(2)}) copy-start(bf16[448,1024]{0,1:T(8,128)(2,1)} %all-reduce.2.cloned.1.call-done) | copy-start | bytes 2752516
  379.4 43.1 %all-to-all-start = ((bf16[8,2,57344]{2,1,0:T(2,128)(2,1)}), bf16[8,2,57344]{2,1,0:T(2,128)(2,1)}, u32[]{:S(2)}, u32[]{:S(2)}) async-start(bf16[8,2,57344]{2,1,0:T(2,128)(2,1)} %reshape.57), calls=%async_computation | async-start | bytes 3670016 | tf_op jit(solution)/shard_map/all_to_all | solution.py:101
  435.4 2.6 copy-start.2
  438.0 3.1 copy-start.1
Sparse Core Ops, SparseCore 0:
  62.0 200.6 reduce-scatter.3
  265.7 35.3 all-reduce.1
